TPU v7x, 32 devices: a whole 2x2x4 slice. The times are simulated.
32 devices in a mesh: ctx: 4 (over x, core), section: 8 (over z, y).
Axes of the slice: x: 2, y: 2, z: 4, core: 2. Of those that a mesh axis runs over, the one named last changes fastest.
Arguments:
- query_in: bfloat16 [8, 2, 512, 1024], P('section', None, 'ctx'), may hold values from -200 to 200
- key_in: bfloat16 [8, 2, 512, 128], P('section', None, 'ctx'), may hold values from -5 to 5
- value_in: bfloat16 [8, 2, 512, 128], P('section', None, 'ctx'), may hold values from -24 to 24
- forward_out: bfloat16 [8, 2, 512, 1024], P('section', None, 'ctx'), may hold values from -6 to 6
- log_sum: float32 [8, 2, 8, 512], P('section', None, None, 'ctx'), as said below
- grad_out: bfloat16 [8, 2, 512, 1024], P('section', None, 'ctx'), may hold values from -6 to 6
- block_order: int32 [8], replicated, may hold values from 0 to 7, each once
Outputs:
- grad_query: bfloat16 [8, 2, 512, 1024], P('section', None, 'ctx')
- grad_key: bfloat16 [8, 2, 512, 128], P('section', None, 'ctx')
- grad_value: bfloat16 [8, 2, 512, 128], P('section', None, 'ctx')
Inputs may be any that keep to these rules, and one draw needn't show every extreme that they name: For every layer, micro-batch, head and row, log_sum is at least the logarithm of the sum of exp(score) over all key rows of that row's window, masked or not. block_order is a permutation: slot j, rows j * 64 to j * 64 + 63 of the token dimension, holds sequence positions block_order[j] * 64 onward in order.
All inputs are finite; a program needn't handle non-finite values.
Results may differ from a plain program's by a relative error of at most 0.008.
Values may be sent and summed in bfloat16 or wider, within the bound.
A program may use at most 64 MiB of HBM per device.

v0:
```python
import functools
import math

import jax
import jax.numpy as jnp
from jax import lax
from jax.experimental import pallas as pl
from jax.experimental.pallas import tpu as pltpu
from jax.sharding import PartitionSpec as P

WINDOW = 3
LOG2E = math.log2(math.e)
HIDE = -1e30


def dot(a, b, dims):
    return lax.dot_general(a, b, (dims, ((), ())), preferred_element_type=jnp.float32)


def kernel(
    members, sections, blocks,
    order_ref, q_hbm, k_hbm, v_hbm, fo_hbm, go_hbm, log_hbm,
    dq_hbm, dk_hbm, dv_hbm,
    q, fo, go, logs, kv, bias, dq, passed, own, part, back, kv_out,
    q_sem, fo_sem, go_sem, log_sem, kv_sem,
    kv_send, kv_recv, part_send, part_recv, hop_send, hop_recv, dq_sem, kv_out_sem,
):
    micro, rows, width = q.shape
    head = kv.shape[-1]
    chunks, _, wide = passed.shape
    group = wide // head
    span = group * rows
    factor = 1.0 / math.sqrt(head)
    me = lax.axis_index("ctx")
    sec = lax.axis_index("section")
    peer = lambda offset: {"ctx": lax.rem(me + offset + members, members)}
    below = {"section": jnp.maximum(sec - 1, 0)}
    above = {"section": jnp.minimum(sec + 1, sections - 1)}
    has_below = sec > 0
    has_above = sec < sections - 1

    kv_loads, loads = [], []
    for m in range(micro):
        for which, source in enumerate((k_hbm, v_hbm)):
            copy = pltpu.make_async_copy(source.at[0, m], kv.at[m, 0, which], kv_sem.at[m, which])
            copy.start()
            kv_loads.append(copy)
    for m in range(micro):
        now = [
            pltpu.make_async_copy(log_hbm.at[0, m], logs.at[m], log_sem.at[m]),
            pltpu.make_async_copy(q_hbm.at[0, m], q.at[m], q_sem.at[m]),
            pltpu.make_async_copy(go_hbm.at[0, m], go.at[m], go_sem.at[m]),
            pltpu.make_async_copy(fo_hbm.at[0, m], fo.at[m], fo_sem.at[m]),
        ]
        for copy in now:
            copy.start()
        loads.append(now)

    barrier = pltpu.get_barrier_semaphore()
    near = sorted({o % members for o in range(1 - WINDOW, WINDOW)} - {0})
    for o in near:
        pl.semaphore_signal(barrier, inc=1, device_id=peer(o), device_id_type=pl.DeviceIdType.MESH)

    @pl.when(has_below)
    def _():
        pl.semaphore_signal(barrier, inc=1, device_id=below, device_id_type=pl.DeviceIdType.MESH)

    @pl.when(has_above)
    def _():
        pl.semaphore_signal(barrier, inc=1, device_id=above, device_id_type=pl.DeviceIdType.MESH)

    half = members * rows // blocks
    per = rows // half
    lane = lax.broadcasted_iota(jnp.int32, (half, rows), 1)
    down = lax.broadcasted_iota(jnp.int32, (half, rows), 0)
    q_place = lax.rem(lane, half)
    for b in range(per):
        base = order_ref[me * per + b] * half
        q_place = q_place + jnp.where(lane // half == b, base, 0)
    for o in range(WINDOW):
        source = lax.rem(me - o + members, members)
        for b in range(per):
            k_place = down + order_ref[source * per + b] * half
            tile = jnp.where(k_place <= q_place, 0.0, HIDE)
            for g in range(group):
                bias[pl.ds(o * rows + b * half, half), pl.ds(g * rows, rows)] = tile

    @pl.when(jnp.logical_not(has_above))
    def _():
        passed[...] = jnp.zeros_like(passed)

    pl.semaphore_wait(barrier, len(near) + has_below.astype(jnp.int32) + has_above.astype(jnp.int32))

    def send_kv(m):
        copies = []
        for o in range(WINDOW - 1, 0, -1):
            copy = pltpu.make_async_remote_copy(
                src_ref=kv.at[m, 0], dst_ref=kv.at[m, o],
                send_sem=kv_send.at[m, o - 1], recv_sem=kv_recv.at[m, o - 1],
                device_id=peer(o), device_id_type=pl.DeviceIdType.MESH,
            )
            copy.start()
            copies.append(copy)
        return copies

    kv_loads[0].wait()
    kv_loads[1].wait()
    kv_copies = [send_kv(0)]

    ones = jnp.ones((8, head), jnp.bfloat16)
    hops, dq_outs, part_copies = [], [], []

    def split(block):
        return jnp.concatenate([block[:, g * head:(g + 1) * head] for g in range(group)], axis=0)

    for m in range(micro):
        for copy in loads[m]:
            copy.wait()
        for copy in kv_copies[m]:
            copy.wait_recv()
        if m == 0:
            for copy in kv_loads[2:]:
                copy.wait()
            for later in range(1, micro):
                kv_copies.append(send_kv(later))
        keys = jnp.concatenate([kv[m, o, 0] for o in range(WINDOW)], axis=0)
        values = jnp.concatenate([kv[m, o, 1] for o in range(WINDOW)], axis=0)
        dk_total = dv_total = None
        for c in range(chunks):
            cols = pl.ds(c * wide, wide)
            queries = split(q[m, :, cols])
            upstream = go[m, :, cols]
            if m > 0:
                if m == 1:
                    @pl.when(has_above)
                    def _(c=c):
                        hop(c).wait_recv()
                upstream = (
                    upstream.astype(jnp.float32) + passed[c].astype(jnp.float32)
                ).astype(jnp.bfloat16)
            upstream = split(upstream)
            product = upstream.astype(jnp.float32) * split(fo[m, :, cols]).astype(jnp.float32)
            high = product.astype(jnp.bfloat16)
            low = (product - high.astype(jnp.float32)).astype(jnp.bfloat16)
            row_dot = (dot(ones, high, ((1,), (1,))) + dot(ones, low, ((1,), (1,))))[0:1]
            log_row = jnp.concatenate(
                [logs[m, pl.ds(c * group + g, 1), :] for g in range(group)], axis=1
            ) * LOG2E
            scores = dot(keys, queries, ((1,), (1,)))
            probs = jnp.exp2(scores * (factor * LOG2E) - log_row + bias[...])
            grad_probs = dot(values, upstream, ((1,), (1,)))
            grad_scores = (probs * (grad_probs - row_dot)).astype(jnp.bfloat16)
            grad_query = dot(grad_scores, keys, ((0,), (0,))) * factor
            for g in range(group):
                dq[m, c, :, pl.ds(g * head, head)] = grad_query[g * rows:(g + 1) * rows].astype(jnp.bfloat16)
            if m == 0:
                def hop(c):
                    return pltpu.make_async_remote_copy(
                        src_ref=dq.at[0, c], dst_ref=passed.at[c],
                        send_sem=hop_send.at[c], recv_sem=hop_recv.at[c],
                        device_id=below, device_id_type=pl.DeviceIdType.MESH,
                    )

                @pl.when(has_below)
                def _(c=c):
                    hop(c).start()
            copy = pltpu.make_async_copy(dq.at[m, c], dq_hbm.at[0, m, :, cols], dq_sem.at[m, c])
            copy.start()
            dq_outs.append(copy)
            dk = dot(grad_scores, queries, ((1,), (0,)))
            dv = dot(probs.astype(jnp.bfloat16), upstream, ((1,), (0,)))
            dk_total = dk if dk_total is None else dk_total + dk
            dv_total = dv if dv_total is None else dv_total + dv
        dk_total = dk_total * factor
        for o in range(WINDOW - 1, 0, -1):
            for which, total in enumerate((dk_total, dv_total)):
                part[m, o - 1, which] = total[o * rows:(o + 1) * rows].astype(jnp.bfloat16)
            copy = pltpu.make_async_remote_copy(
                src_ref=part.at[m, o - 1], dst_ref=back.at[m, o - 1],
                send_sem=part_send.at[m, o - 1], recv_sem=part_recv.at[m, o - 1],
                device_id=peer(-o), device_id_type=pl.DeviceIdType.MESH,
            )
            copy.start()
            part_copies.append((m, o, copy))
        own[m, 0] = dk_total[:rows]
        own[m, 1] = dv_total[:rows]

    kv_outs = []
    for m in range(micro):
        for at, o, copy in part_copies:
            if at == m:
                copy.wait_recv()
        for which, target in enumerate((dk_hbm, dv_hbm)):
            total = own[m, which]
            for o in range(1, WINDOW):
                total = total + back[m, o - 1, which].astype(jnp.float32)
            kv_out[m, which] = total.astype(jnp.bfloat16)
            copy = pltpu.make_async_copy(kv_out.at[m, which], target.at[0, m], kv_out_sem.at[m, which])
            copy.start()
            kv_outs.append(copy)
    for copies in kv_copies:
        for copy in copies:
            copy.wait_send()
    for _, _, copy in part_copies:
        copy.wait_send()

    @pl.when(has_below)
    def _():
        for c in range(chunks):
            hop(c).wait_send()

    for copy in dq_outs + kv_outs:
        copy.wait()


def solution(mesh):
    members = mesh.shape["ctx"]
    sections = mesh.shape["section"]
    in_specs = (
        P("section", None, "ctx", None),
        P("section", None, "ctx", None),
        P("section", None, "ctx", None),
        P("section", None, "ctx", None),
        P("section", None, None, "ctx"),
        P("section", None, "ctx", None),
        P(),
    )
    out_specs = (
        P("section", None, "ctx", None),
        P("section", None, "ctx", None),
        P("section", None, "ctx", None),
    )

    def shards(query_in, key_in, value_in, forward_out, log_sum, grad_out, block_order):
        _, micro, rows, width = query_in.shape
        head = key_in.shape[3]
        heads = width // head
        group = 2 if heads % 2 == 0 else 1
        chunks = heads // group
        wide = group * head
        low, full = jnp.bfloat16, jnp.float32
        dma = pltpu.SemaphoreType.DMA
        others = WINDOW - 1
        return pl.pallas_call(
            functools.partial(kernel, members, sections, block_order.shape[0]),
            out_shape=(
                jax.ShapeDtypeStruct(query_in.shape, low),
                jax.ShapeDtypeStruct(key_in.shape, low),
                jax.ShapeDtypeStruct(value_in.shape, low),
            ),
            in_specs=[pl.BlockSpec(memory_space=pltpu.SMEM)]
            + [pl.BlockSpec(memory_space=pl.ANY)] * 6,
            out_specs=[pl.BlockSpec(memory_space=pl.ANY)] * 3,
            scratch_shapes=[
                pltpu.VMEM((micro, rows, width), low),
                pltpu.VMEM((micro, rows, width), low),
                pltpu.VMEM((micro, rows, width), low),
                pltpu.VMEM((micro, heads, rows), full),
                pltpu.VMEM((micro, WINDOW, 2, rows, head), low),
                pltpu.VMEM((WINDOW * rows, group * rows), full),
                pltpu.VMEM((micro, chunks, rows, wide), low),
                pltpu.VMEM((chunks, rows, wide), low),
                pltpu.VMEM((micro, 2, rows, head), full),
                pltpu.VMEM((micro, others, 2, rows, head), low),
                pltpu.VMEM((micro, others, 2, rows, head), low),
                pltpu.VMEM((micro, 2, rows, head), low),
                dma((micro,)), dma((micro,)), dma((micro,)), dma((micro,)), dma((micro, 2)),
                dma((micro, others)), dma((micro, others)),
                dma((micro, others)), dma((micro, others)),
                dma((chunks,)), dma((chunks,)),
                dma((micro, chunks)), dma((micro, 2)),
            ],
            compiler_params=pltpu.CompilerParams(collective_id=0, has_side_effects=True),
        )(block_order, query_in, key_in, value_in, forward_out, grad_out, log_sum)

    return jax.shard_map(shards, mesh=mesh, in_specs=in_specs, out_specs=out_specs, check_vma=False)
```

profile of v0, /device:TPU:1, one launch (start us, length us, event | category | flops | bytes accessed | tf_op | source)
XLA Modules:
  0.0 24.1 jit_solution(15769902192446167813)
XLA Ops:
  0.6 20.1 %shard_map.94 = (bf16[1,2,128,1024]{3,2,1,0:T(8,128)(2,1)}, bf16[1,2,128,128]{3,2,1,0:T(8,128)(2,1)}, bf16[1,2,128,128]{3,2,1,0:T(8,128)(2,1)}) custom-call(s32[8]{0:T(128)} %order_ref.1, bf16[1,2,128,1024]{3,2,1,0:T(8,128)(2,1)} %q_hbm.1, bf16[1,2,128,128]{3,2,1,0:T(8,128)(2,1)} %k_hbm.1, bf16[1,2,128,128]{3,2,1,0:T(8,128)(2,1)} %v_hbm.1, ...), custom_call_target="tpu_custom_call" | custom-call | tf_op jit(solution)/shard_map/pallas_call | solution.py:244
  20.7 0.0 copy-start.1
  20.7 1.9 %copy.13 = bf16[1,2,128,1024]{3,2,1,0:T(8,128)(2,1)} copy(bf16[1,2,128,1024]{3,2,1,0:T(8,128)(2,1)} %get-tuple-element.6) | data formatting | bytes 1048576
  22.6 0.0 copy-done.1
  22.6 0.0 copy-start
  22.7 0.6 %copy.14 = bf16[1,2,128,128]{3,2,1,0:T(8,128)(2,1)} copy(bf16[1,2,128,128]{3,2,1,0:T(8,128)(2,1)S(1)} %copy-done.1) | data formatting | bytes 131072
  23.3 0.2 copy-done
  23.5 0.6 %copy.15 = bf16[1,2,128,128]{3,2,1,0:T(8,128)(2,1)} copy(bf16[1,2,128,128]{3,2,1,0:T(8,128)(2,1)S(1)} %copy-done) | data formatting | bytes 131072
Async XLA Ops:
  20.7 1.9 %copy-start.1 = (bf16[1,2,128,128]{3,2,1,0:T(8,128)(2,1)S(1)}, bf16[1,2,128,128]{3,2,1,0:T(8,128)(2,1)}, u32[]{:S(2)}) copy-start(bf16[1,2,128,128]{3,2,1,0:T(8,128)(2,1)} %get-tuple-element.7) | copy-start | bytes 196612
  22.6 0.9 %copy-start = (bf16[1,2,128,128]{3,2,1,0:T(8,128)(2,1)S(1)}, bf16[1,2,128,128]{3,2,1,0:T(8,128)(2,1)}, u32[]{:S(2)}) copy-start(bf16[1,2,128,128]{3,2,1,0:T(8,128)(2,1)} %get-tuple-element.8) | copy-start | bytes 196612
where the time goes:
time: 24.3 us; the launch traced here: 24.1 us
  Pallas kernels  20.1 us (83%)
  local copies, waits for them, and re-layouts  3.4 us (14%)
  between operations  0.65 us (3%)
    pallas_call x1, Pallas kernels, shards(): pl.pallas_call(functools.partial(kernel, members, sections, block_order.s...  20.1 us
    unnamed x7, local copies, waits for them, and re-layouts  3.4 us

commit v1 on v0

--- a/solution.py
+++ b/solution.py
@@ -20,10 +20,10 @@
 def kernel(
     members, sections, blocks,
     order_ref, q_hbm, k_hbm, v_hbm, fo_hbm, go_hbm, log_hbm,
-    dq_hbm, dk_hbm, dv_hbm,
-    q, fo, go, logs, kv, bias, dq, passed, own, part, back, kv_out,
+    dq, kv_out,
+    q, fo, go, logs, kv, bias, passed, own, part, back,
     q_sem, fo_sem, go_sem, log_sem, kv_sem,
-    kv_send, kv_recv, part_send, part_recv, hop_send, hop_recv, dq_sem, kv_out_sem,
+    kv_send, kv_recv, part_send, part_recv, hop_send, hop_recv,
 ):
     micro, rows, width = q.shape
     head = kv.shape[-1]
@@ -108,7 +108,7 @@
     kv_copies = [send_kv(0)]
 
     ones = jnp.ones((8, head), jnp.bfloat16)
-    hops, dq_outs, part_copies = [], [], []
+    part_copies = []
 
     def split(block):
         return jnp.concatenate([block[:, g * head:(g + 1) * head] for g in range(group)], axis=0)
@@ -164,9 +164,6 @@
                 @pl.when(has_below)
                 def _(c=c):
                     hop(c).start()
-            copy = pltpu.make_async_copy(dq.at[m, c], dq_hbm.at[0, m, :, cols], dq_sem.at[m, c])
-            copy.start()
-            dq_outs.append(copy)
             dk = dot(grad_scores, queries, ((1,), (0,)))
             dv = dot(probs.astype(jnp.bfloat16), upstream, ((1,), (0,)))
             dk_total = dk if dk_total is None else dk_total + dk
@@ -185,19 +182,15 @@
         own[m, 0] = dk_total[:rows]
         own[m, 1] = dv_total[:rows]
 
-    kv_outs = []
     for m in range(micro):
         for at, o, copy in part_copies:
             if at == m:
                 copy.wait_recv()
-        for which, target in enumerate((dk_hbm, dv_hbm)):
+        for which in range(2):
             total = own[m, which]
             for o in range(1, WINDOW):
                 total = total + back[m, o - 1, which].astype(jnp.float32)
             kv_out[m, which] = total.astype(jnp.bfloat16)
-            copy = pltpu.make_async_copy(kv_out.at[m, which], target.at[0, m], kv_out_sem.at[m, which])
-            copy.start()
-            kv_outs.append(copy)
     for copies in kv_copies:
         for copy in copies:
             copy.wait_send()
@@ -209,7 +202,22 @@
         for c in range(chunks):
             hop(c).wait_send()
 
-    for copy in dq_outs + kv_outs:
+
+def writer(dq, kv_out, dq_hbm, dk_hbm, dv_hbm, dq_sem, kv_sem):
+    micro, chunks, _, wide = dq.shape
+    copies = []
+    for m in range(micro):
+        for c in range(chunks):
+            copies.append(pltpu.make_async_copy(
+                dq.at[m, c], dq_hbm.at[0, m, :, pl.ds(c * wide, wide)], dq_sem.at[m, c]
+            ))
+        for which, target in enumerate((dk_hbm, dv_hbm)):
+            copies.append(pltpu.make_async_copy(
+                kv_out.at[m, which], target.at[0, m], kv_sem.at[m, which]
+            ))
+    for copy in copies:
+        copy.start()
+    for copy in copies:
         copy.wait()
 
 
@@ -241,16 +249,15 @@
         low, full = jnp.bfloat16, jnp.float32
         dma = pltpu.SemaphoreType.DMA
         others = WINDOW - 1
-        return pl.pallas_call(
+        dq, kv_out = pl.pallas_call(
             functools.partial(kernel, members, sections, block_order.shape[0]),
             out_shape=(
-                jax.ShapeDtypeStruct(query_in.shape, low),
-                jax.ShapeDtypeStruct(key_in.shape, low),
-                jax.ShapeDtypeStruct(value_in.shape, low),
+                pltpu.VMEM((micro, chunks, rows, wide), low),
+                pltpu.VMEM((micro, 2, rows, head), low),
             ),
             in_specs=[pl.BlockSpec(memory_space=pltpu.SMEM)]
             + [pl.BlockSpec(memory_space=pl.ANY)] * 6,
-            out_specs=[pl.BlockSpec(memory_space=pl.ANY)] * 3,
+            out_specs=[pl.BlockSpec(memory_space=pltpu.VMEM)] * 2,
             scratch_shapes=[
                 pltpu.VMEM((micro, rows, width), low),
                 pltpu.VMEM((micro, rows, width), low),
@@ -258,19 +265,27 @@
                 pltpu.VMEM((micro, heads, rows), full),
                 pltpu.VMEM((micro, WINDOW, 2, rows, head), low),
                 pltpu.VMEM((WINDOW * rows, group * rows), full),
-                pltpu.VMEM((micro, chunks, rows, wide), low),
                 pltpu.VMEM((chunks, rows, wide), low),
                 pltpu.VMEM((micro, 2, rows, head), full),
                 pltpu.VMEM((micro, others, 2, rows, head), low),
                 pltpu.VMEM((micro, others, 2, rows, head), low),
-                pltpu.VMEM((micro, 2, rows, head), low),
                 dma((micro,)), dma((micro,)), dma((micro,)), dma((micro,)), dma((micro, 2)),
                 dma((micro, others)), dma((micro, others)),
                 dma((micro, others)), dma((micro, others)),
                 dma((chunks,)), dma((chunks,)),
-                dma((micro, chunks)), dma((micro, 2)),
             ],
             compiler_params=pltpu.CompilerParams(collective_id=0, has_side_effects=True),
         )(block_order, query_in, key_in, value_in, forward_out, grad_out, log_sum)
+        return pl.pallas_call(
+            writer,
+            out_shape=(
+                jax.ShapeDtypeStruct(query_in.shape, low),
+                jax.ShapeDtypeStruct(key_in.shape, low),
+                jax.ShapeDtypeStruct(value_in.shape, low),
+            ),
+            in_specs=[pl.BlockSpec(memory_space=pltpu.VMEM)] * 2,
+            out_specs=[pl.BlockSpec(memory_space=pl.ANY)] * 3,
+            scratch_shapes=[dma((micro, chunks)), dma((micro, 2))],
+        )(*(pltpu.with_memory_space_constraint(x, pltpu.VMEM) for x in (dq, kv_out)))
 
     return jax.shard_map(shards, mesh=mesh, in_specs=in_specs, out_specs=out_specs, check_vma=False)

time: 24.3 us -> 21.1 us (0.87)
  local copies, waits for them, and re-layouts: 3.4 us -> 0 us
    unnamed x7 -> x0, local copies, waits for them, and re-layouts: 3.4 us -> none
    pallas_call x0 -> x1, Pallas kernels: none -> 0.93 us  [shards(): pl.pallas_call(writer, out_shape=(jax.ShapeDtypeStruct(query_in.shape, lo...]
    pallas_call x1, Pallas kernels: 20.1 us -> 19.4 us  [shards(): pl.pallas_call(functools.partial(kernel, members, sections, block_order.s...]
where the time goes in v1:
time: 21.1 us; the launch traced here: 20.9 us
  Pallas kernels  20.3 us (96%)
  between operations  0.64 us (3%)
    pallas_call x1, Pallas kernels, shards(): pl.pallas_call(functools.partial(kernel, members, sections, block_order.s...  19.4 us
    pallas_call x1, Pallas kernels, shards(): pl.pallas_call(writer, out_shape=(jax.ShapeDtypeStruct(query_in.shape, lo...  0.93 us

profile of v1, /device:TPU:1, one launch (start us, length us, event | category | flops | bytes accessed | tf_op | source)
XLA Modules:
  0.0 20.9 jit_solution(3003218030649234933)
XLA Ops:
  0.6 19.4 %shard_map.94 = (bf16[2,4,128,256]{3,2,1,0:T(8,128)(2,1)S(1)}, bf16[2,2,128,128]{3,2,1,0:T(8,128)(2,1)S(1)}) custom-call(s32[8]{0:T(128)} %order_ref.1, bf16[1,2,128,1024]{3,2,1,0:T(8,128)(2,1)} %q_hbm.1, bf16[1,2,128,128]{3,2,1,0:T(8,128)(2,1)} %k_hbm.1, bf16[1,2,128,128]{3,2,1,0:T(8,128)(2,1)} %v_hbm.1, bf16[1,2,128,1024]{3,2,1,0:T(8,128)(2,1)} %fo_hbm.1, ...), custom_call_target="tpu_custom_call" | custom-call | tf_op jit(solution)/shard_map/pallas_call | solution.py:252
  20.0 0.9 %shard_map.95 = (bf16[1,2,128,1024]{3,2,1,0:T(8,128)(2,1)}, bf16[1,2,128,128]{3,2,1,0:T(8,128)(2,1)}, bf16[1,2,128,128]{3,2,1,0:T(8,128)(2,1)}) custom-call(bf16[2,4,128,256]{3,2,1,0:T(8,128)(2,1)S(1)} %get-tuple-element.5.dq, bf16[2,2,128,128]{3,2,1,0:T(8,128)(2,1)S(1)} %get-tuple-element.6.kv_out), custom_call_target="tpu_custom_call" | custom-call | tf_op jit(solution)/shard_map/pallas_call | solution.py:279
